TPU v7x, 16 devices: a 4x2x1 block of a 4x4x8 slice. The times are simulated.
16 devices in a mesh: dp: 4 (over y, z, core), tp: 4 (over x).
Axes of the slice: x: 4, y: 2, z: 1, core: 2. Of those that a mesh axis runs over, the one named last changes fastest.
The devices are a block of a 4x4x8 slice.
Arguments:
- x: bfloat16 [5632, 3072], P(('dp', 'tp')), parts along dimension 0
- w_gate: bfloat16 [3072, 8192], P(None, 'tp')
- w_up: bfloat16 [3072, 8192], P(None, 'tp')
- w_down: bfloat16 [8192, 3072], P('tp')
Outputs:
- output: bfloat16 [5632, 3072], P(('dp', 'tp')), parts along dimension 0
There are 4 independent parts. A program takes and returns all parts, laid end to end along the dimension named above; an argument that names none is the same for every part.
All inputs are finite; a program needn't handle non-finite values.
Results may differ from a plain program's by a relative error of at most 0.016.
Values are sent between devices in bfloat16 or wider.
A program may use at most 768 MiB of HBM per device.

v0:
```python
import jax
import jax.numpy as jnp
from jax import lax
from jax.sharding import PartitionSpec as P


def solution(mesh):
    def step(x, w_gate, w_up, w_down):
        rows = lax.all_gather(x, "tp", axis=0, tiled=True)
        gate = jnp.dot(rows, w_gate, preferred_element_type=jnp.float32)
        up = jnp.dot(rows, w_up, preferred_element_type=jnp.float32)
        hidden = (jax.nn.silu(gate) * up).astype(jnp.bfloat16)
        term = jnp.dot(hidden, w_down, preferred_element_type=jnp.float32).astype(jnp.bfloat16)
        return lax.psum_scatter(term, "tp", scatter_dimension=0, tiled=True)

    return jax.shard_map(
        step,
        mesh=mesh,
        in_specs=(P(("dp", "tp"), None), P(None, "tp"), P(None, "tp"), P("tp", None)),
        out_specs=P(("dp", "tp"), None),
        check_vma=False,
    )
```

profile of v0, /device:TPU:112, one launch (start us, length us, event | category | flops | bytes accessed | tf_op | source)
XLA Modules:
  0.0 248.5 jit_solution(3444367157514199162)
XLA Ops:
  6.5 0.0 all-gather.2.cloned.1.call-start
  6.6 0.7 all-gather.2.cloned.1.call-update
  7.3 0.1 reduce-scatter.2.cloned.1.call-start
  7.4 85.9 %all-gather.2.cloned.1.call-done = bf16[1408,3072]{1,0:T(8,128)(2,1)} async-done(((bf16[352,3072]{1,0:T(8,128)(2,1)}), bf16[1408,3072]{1,0:T(8,128)(2,1)}) %all-gather.2.cloned.1.call-update) | async-done | bytes 8650768 | tf_op jit(solution)/shard_map/all_gather | solution.py:9
  93.3 0.0 copy-start
  93.3 0.0 slice-start
  93.3 0.0 slice-start.1
  93.3 24.8 %fusion = f32[1408,2048]{1,0:T(8,128)} fusion(bf16[1408,3072]{1,0:T(8,128)(2,1)} %all-gather.2.cloned.1.call-done, bf16[3072,2048]{1,0:T(8,128)(2,1)} %param.5), kind=kOutput, calls=%fused_computation.2 | convolution fusion | flops 17716740096 | bytes 32768000 | tf_op jit(solution)/shard_map/dot_general | solution.py:10
  118.1 0.0 copy-done
  118.1 0.0 slice-start.2
  118.1 23.4 %multiply_convert_fusion = bf16[1408,2048]{1,0:T(8,128)(2,1)S(1)} fusion(f32[1408,2048]{1,0:T(8,128)} %fusion, bf16[1408,3072]{1,0:T(8,128)(2,1)S(1)} %copy-done, bf16[3072,2048]{1,0:T(8,128)(2,1)} %param.6), kind=kOutput, calls=%fused_computation | convolution fusion | flops 17734041600 | bytes 38535168 | tf_op jit(solution)/shard_map/dot_general | solution.py:11
  141.4 0.0 slice-done
  141.4 0.0 slice-done.1
  141.5 0.0 slice-done.2
  141.5 20.5 %convolution_convert_fusion = bf16[1408,3072]{1,0:T(8,128)(2,1)} fusion(bf16[1408,2048]{1,0:T(8,128)(2,1)S(1)} %multiply_convert_fusion, bf16[2048,3072]{1,0:T(8,128)(2,1)S(1)} %bitcast.7), kind=kOutput, calls=%fused_computation.1 | convolution fusion | flops 17721065472 | bytes 27000832 | tf_op jit(solution)/shard_map/dot_general | solution.py:13
  162.0 0.1 reduce-scatter.2.cloned.1.call-update
  162.0 79.7 %reduce-scatter.2.cloned.1.call-done = bf16[352,3072]{1,0:T(8,128)(2,1)} async-done(((bf16[1408,3072]{1,0:T(8,128)(2,1)}), bf16[352,3072]{1,0:T(8,128)(2,1)}) %reduce-scatter.2.cloned.1.call-update) | async-done | bytes 2162704 | tf_op jit(solution)/shard_map/reduce_scatter | solution.py:14
  (1 shorter events, 0.0 us)
Async XLA Ops:
  6.5 86.7 %all-gather.2.cloned.1.call-start = ((), (), s32[]{:S(2)}) async-start(), calls=%async_computation.1 | async-start | bytes 10813440 | tf_op jit(solution)/shard_map/all_gather | solution.py:9
  7.3 234.4 %reduce-scatter.2.cloned.1.call-start = ((), (), s32[]{:S(2)}) async-start(), calls=%async_computation.2 | async-start | bytes 10813440 | tf_op jit(solution)/shard_map/reduce_scatter | solution.py:14
  93.3 24.8 %copy-start = (bf16[1408,3072]{1,0:T(8,128)(2,1)S(1)}, bf16[1408,3072]{1,0:T(8,128)(2,1)}, u32[]{:S(2)}) copy-start(bf16[1408,3072]{1,0:T(8,128)(2,1)} %all-gather.2.cloned.1.call-done) | copy-start | bytes 25952260
  93.3 48.2 %slice-start = ((s8[12582912]{0:T(1024)(128)(4,1)}), s8[4194304]{0:T(1024)(128)(4,1)S(1)}, s32[]{:S(2)}) async-start(s8[12582912]{0:T(1024)(128)(4,1)} %bitcast.6), calls=%async_computation.3 | async-start | bytes 8388608
  93.3 48.2 %slice-start.1 = ((s8[12582912]{0:T(1024)(128)(4,1)}), s8[4194304]{0:T(1024)(128)(4,1)S(1)}, s32[]{:S(2)}) async-start(s8[12582912]{0:T(1024)(128)(4,1)} %bitcast.6), calls=%async_computation.4 | async-start | bytes 8388608
  118.1 23.4 %slice-start.2 = ((s8[12582912]{0:T(1024)(128)(4,1)}), s8[4194304]{0:T(1024)(128)(4,1)S(1)}, s32[]{:S(2)}) async-start(s8[12582912]{0:T(1024)(128)(4,1)} %bitcast.6), calls=%async_computation.5 | async-start | bytes 8388608
Sparse Core Ops, SparseCore 0:
  8.9 84.3 all-gather.1
  162.2 79.4 reduce-scatter.1
where the time goes:
time: 249 us
  waiting for transfers between devices  166 us (67%)
  matrix products  68.7 us (28%)
  between operations  13.5 us (5%)
    all_gather x1, waiting for transfers between devices, step(): rows = lax.all_gather(x, 'tp', axis=0, tiled=True)  85.9 us
    reduce_scatter x1, waiting for transfers between devices, step(): return lax.psum_scatter(term, 'tp', scatter_dimension=0, tiled=True)  79.7 us
    dot_general x1, matrix products, step(): gate = jnp.dot(rows, w_gate, preferred_element_type=jnp.float32)  24.8 us
    dot_general x1, matrix products, step(): up = jnp.dot(rows, w_up, preferred_element_type=jnp.float32)  23.4 us
    dot_general x1, matrix products, step(): jnp.dot(hidden, w_down, preferred_element_type=jnp.float32)  20.5 us
  transfers between devices with their start and end apart: 2, of which 2 were waited for; matrix products, arithmetic and copies ran while one was open for 0% of the time, Pallas kernels for 0%

commit v1 on v0

v1 whole, which is shorter than its diff:
```python
import functools

import jax
import jax.numpy as jnp
from jax import lax
from jax.experimental import pallas as pl
from jax.experimental.pallas import tpu as pltpu
from jax.sharding import PartitionSpec as P

MESH = pl.DeviceIdType.MESH
FF_TILE = 256
OUT_TILE = 512


def kernel(
    n, x_ref, wg_ref, wu_ref, wd_ref, y_ref,
    xg, vg, vu, vd, acc, hid, hid2, r_dir, r_hop, r_run,
    x_sem, wgu_sem, wd_sem, y_sem, ag_send, ag_recv, rs_send, rs_recv,
):
    rows, d = x_ref.shape
    ff = vg.shape[1]
    half = rows // 2
    n_ff, n_out = ff // FF_TILE, d // OUT_TILE
    me = lax.axis_index("tp")
    right, left = lax.rem(me + 1, n), lax.rem(me + n - 1, n)
    first, second = pl.ds(0, half), pl.ds(half, half)

    barrier = pltpu.get_barrier_semaphore()
    for neighbour in (left, right):
        pl.semaphore_signal(barrier, inc=1, device_id={"tp": neighbour}, device_id_type=MESH)

    def ff_cols(j):
        return pl.ds(pl.multiple_of(j * FF_TILE, FF_TILE), FF_TILE)

    def out_cols(j):
        return pl.ds(pl.multiple_of(j * OUT_TILE, OUT_TILE), OUT_TILE)

    def load_gate(j):
        return pltpu.make_async_copy(wg_ref.at[:, ff_cols(j)], vg.at[:, ff_cols(j)], wgu_sem.at[0, j])

    def load_up(j):
        return pltpu.make_async_copy(wu_ref.at[:, ff_cols(j)], vu.at[:, ff_cols(j)], wgu_sem.at[1, j])

    def load_down(j):
        return pltpu.make_async_copy(wd_ref.at[:, out_cols(j)], vd.at[:, out_cols(j)], wd_sem.at[j])

    load_x = pltpu.make_async_copy(x_ref, xg.at[0], x_sem)
    load_x.start()

    @pl.loop(0, n_ff)
    def _(j):
        load_gate(j).start()
        load_up(j).start()

    @pl.loop(0, n_out)
    def _(j):
        load_down(j).start()

    def remote(src, dst, sends, recvs, i, to):
        return pltpu.make_async_remote_copy(
            src_ref=src, dst_ref=dst, send_sem=sends.at[i], recv_sem=recvs.at[i],
            device_id={"tp": to}, device_id_type=MESH,
        )

    own = [
        remote(x_ref.at[first], xg.at[1, first], ag_send, ag_recv, 0, right),
        remote(x_ref.at[second], xg.at[1, second], ag_send, ag_recv, 1, left),
        remote(x_ref.at[second], xg.at[2, first], ag_send, ag_recv, 2, right),
        remote(x_ref.at[first], xg.at[2, second], ag_send, ag_recv, 3, left),
    ]
    forward = [
        remote(xg.at[1, first], xg.at[3, first], ag_send, ag_recv, 4, right),
        remote(xg.at[1, second], xg.at[3, second], ag_send, ag_recv, 5, left),
    ]

    def tile_send(src, src_half, dst, dst_half, kind, j, to):
        return pltpu.make_async_remote_copy(
            src_ref=src.at[src_half, out_cols(j)], dst_ref=dst.at[dst_half, out_cols(j)],
            send_sem=rs_send.at[kind, j], recv_sem=rs_recv.at[kind, j],
            device_id={"tp": to}, device_id_type=MESH,
        )

    def direct(j):
        return (tile_send(xg.at[0], first, r_dir, first, 0, j, left),
                tile_send(xg.at[0], second, r_dir, second, 1, j, right))

    def hop(j):
        return (tile_send(xg.at[3], second, r_hop, first, 2, j, left),
                tile_send(xg.at[3], first, r_hop, second, 3, j, right))

    def running(j):
        return (tile_send(xg.at[2], first, r_run, second, 4, j, left),
                tile_send(xg.at[2], second, r_run, first, 5, j, right))

    def start(copies):
        for copy in copies:
            copy.start()

    def recv(copies):
        for copy in copies:
            copy.wait_recv()

    def sent(copies):
        for copy in copies:
            copy.wait_send()

    pl.semaphore_wait(barrier, 2)
    start(own)

    def hidden(group, out, loading):
        @pl.loop(0, n_ff)
        def _(j):
            if loading:
                load_gate(j).wait()
                load_up(j).wait()
            gate = jnp.dot(xg[group], vg[:, ff_cols(j)], preferred_element_type=jnp.float32)
            up = jnp.dot(xg[group], vu[:, ff_cols(j)], preferred_element_type=jnp.float32)
            out[:, ff_cols(j)] = (jax.nn.silu(gate) * up).astype(out.dtype)

    def down(src, j):
        return jnp.dot(src[...], vd[:, out_cols(j)], preferred_element_type=jnp.float32)

    load_x.wait()
    hidden(0, hid, True)

    @pl.loop(0, n_out)
    def _(j):
        load_down(j).wait()
        acc[:, out_cols(j)] = down(hid, j)

    recv(own[:2])
    start(forward)
    hidden(1, hid, False)

    @pl.loop(0, n_out)
    def _(j):
        xg[0, :, out_cols(j)] = down(hid, j).astype(xg.dtype)

        @pl.when(j > 0)
        def _():
            start(direct(j - 1))

    recv(own[2:])
    start(direct(n_out - 1))
    hidden(2, hid2, False)

    recv(forward)
    hidden(3, hid, False)

    @pl.loop(0, n_out)
    def _(j):
        xg[3, :, out_cols(j)] = down(hid, j).astype(xg.dtype)

        @pl.when(j > 0)
        def _():
            start(hop(j - 1))

    recv(direct(0))
    start(hop(n_out - 1))

    @pl.loop(0, n_out)
    def _(j):
        @pl.when(j > 0)
        def _():
            recv(direct(j))

        acc[:, out_cols(j)] = acc[:, out_cols(j)] + r_dir[:, out_cols(j)].astype(jnp.float32)

    @pl.loop(0, n_out)
    def _(j):
        recv(hop(j))
        total = down(hid2, j) + r_hop[:, out_cols(j)].astype(jnp.float32)
        xg[2, :, out_cols(j)] = total.astype(xg.dtype)

        @pl.when(j > 0)
        def _():
            start(running(j - 1))

    sent(forward)
    start(running(n_out - 1))

    def store(j):
        return pltpu.make_async_copy(xg.at[1, :, out_cols(j)], y_ref.at[:, out_cols(j)], y_sem.at[j])

    @pl.loop(0, n_out)
    def _(j):
        recv(running(j))
        total = acc[:, out_cols(j)] + r_run[:, out_cols(j)].astype(jnp.float32)
        xg[1, :, out_cols(j)] = total.astype(xg.dtype)
        store(j).start()

    sent(own)

    @pl.loop(0, n_out)
    def _(j):
        sent(direct(j))
        sent(hop(j))
        sent(running(j))
        store(j).wait()


def solution(mesh):
    n = mesh.shape["tp"]

    def step(x, w_gate, w_up, w_down):
        rows, d = x.shape
        ff = w_gate.shape[1]
        n_ff, n_out = ff // FF_TILE, d // OUT_TILE
        bf16, f32 = jnp.bfloat16, jnp.float32
        block = pltpu.VMEM((rows, d), bf16)
        sem = pltpu.SemaphoreType.DMA
        return pl.pallas_call(
            functools.partial(kernel, n),
            out_shape=jax.ShapeDtypeStruct((rows, d), x.dtype),
            in_specs=[pl.BlockSpec(memory_space=pl.ANY)] * 4,
            out_specs=pl.BlockSpec(memory_space=pl.ANY),
            scratch_shapes=[
                pltpu.VMEM((4, rows, d), bf16),
                pltpu.VMEM((d, ff), bf16), pltpu.VMEM((d, ff), bf16), pltpu.VMEM((ff, d), bf16),
                pltpu.VMEM((rows, d), f32),
                pltpu.VMEM((rows, ff), bf16), pltpu.VMEM((rows, ff), bf16),
                block, block, block,
                sem, sem((2, n_ff)), sem((n_out,)), sem((n_out,)),
                sem((6,)), sem((6,)), sem((6, n_out)), sem((6, n_out)),
            ],
            compiler_params=pltpu.CompilerParams(
                collective_id=0, has_side_effects=True, vmem_limit_bytes=67_043_328
            ),
        )(x, w_gate, w_up, w_down)

    return jax.shard_map(
        step,
        mesh=mesh,
        in_specs=(P(("dp", "tp"), None), P(None, "tp"), P(None, "tp"), P("tp", None)),
        out_specs=P(("dp", "tp"), None),
        check_vma=False,
    )
```

time: 249 us -> 149 us (0.60)
  waiting for transfers between devices: 166 us -> 0 us
  Pallas kernels: 0 us -> 146 us
  matrix products: 68.7 us -> 0 us
  between operations: 13.5 us -> 0.01 us
  local copies, waits for them, and re-layouts: 0.01 us -> 3.09 us
    pallas_call x0 -> x1, Pallas kernels: none -> 146 us  [step(): pl.pallas_call(functools.partial(kernel, n), out_shape=jax.ShapeDtypeStru...]
    all_gather x1 -> x0, waiting for transfers between devices: 85.9 us -> none  [step(): rows = lax.all_gather(x, 'tp', axis=0, tiled=True)]
    reduce_scatter x1 -> x0, waiting for transfers between devices: 79.7 us -> none  [step(): return lax.psum_scatter(term, 'tp', scatter_dimension=0, tiled=True)]
    dot_general x3 -> x0, matrix products: 68.7 us -> none  [the longest x1 24.8 us: step(): gate = jnp.dot(rows, w_gate, preferred_element_type=jnp.float32)]
    unnamed x8 -> x1, local copies, waits for them, and re-layouts: 0.01 us -> 3.09 us
  transfers between devices with their start and end apart: 2 -> 0, of which waited for: 2 -> 0; matrix products, arithmetic and copies ran while one was open for 0% -> 0% of each run, Pallas kernels for 0% -> 0%
where the time goes in v1:
time: 149 us
  Pallas kernels  146 us (98%)
  local copies, waits for them, and re-layouts  3.09 us (2%)
    pallas_call x1, Pallas kernels, step(): pl.pallas_call(functools.partial(kernel, n), out_shape=jax.ShapeDtypeStru...  146 us
    unnamed x1, local copies, waits for them, and re-layouts  3.09 us

profile of v1, /device:TPU:112, one launch (start us, length us, event | category | flops | bytes accessed | tf_op | source)
XLA Modules:
  0.0 149.1 jit_solution(12644007305509959905)
XLA Ops:
  0.0 146.0 %shard_map.46 = bf16[352,3072]{1,0:T(8,128)(2,1)} custom-call(bf16[352,3072]{1,0:T(8,128)(2,1)} %x_ref.1, bf16[3072,2048]{1,0:T(8,128)(2,1)} %wg_ref.1, bf16[3072,2048]{1,0:T(8,128)(2,1)} %wu_ref.1, bf16[2048,3072]{1,0:T(8,128)(2,1)} %wd_ref.1), custom_call_target="tpu_custom_call" | custom-call | tf_op jit(solution)/shard_map/pallas_call | solution.py:212
  146.0 3.1 %copy.6 = bf16[352,3072]{1,0:T(8,128)(2,1)} copy(bf16[352,3072]{1,0:T(8,128)(2,1)} %shard_map.46) | data formatting | bytes 4325376

commit v2 on v1

v2 whole, which is shorter than its diff:
```python
import functools

import jax
import jax.numpy as jnp
from jax import lax
from jax.experimental import pallas as pl
from jax.experimental.pallas import tpu as pltpu
from jax.sharding import PartitionSpec as P

MESH = pl.DeviceIdType.MESH
FF_TILE = 256
OUT_TILE = 512


def kernel(
    n, x_ref, wg_ref, wu_ref, wd_ref, y_ref,
    xg, vg, vu, vd, acc, hid, hid2, r_dir, r_hop, r_run,
    x_sem, wgu_sem, wd_sem, ag_send, ag_recv, rs_send, dir_recv, hop_recv, run_recv,
):
    rows, d = x_ref.shape
    ff = vg.shape[1]
    half = rows // 2
    n_ff, n_out = ff // FF_TILE, d // OUT_TILE
    me = lax.axis_index("tp")
    right, left = lax.rem(me + 1, n), lax.rem(me + n - 1, n)
    first, second = pl.ds(0, half), pl.ds(half, half)

    barrier = pltpu.get_barrier_semaphore()
    for neighbour in (left, right):
        pl.semaphore_signal(barrier, inc=1, device_id={"tp": neighbour}, device_id_type=MESH)

    def ff_cols(j):
        return pl.ds(pl.multiple_of(j * FF_TILE, FF_TILE), FF_TILE)

    def out_cols(j):
        return pl.ds(pl.multiple_of(j * OUT_TILE, OUT_TILE), OUT_TILE)

    load_x = pltpu.make_async_copy(x_ref, xg.at[0], x_sem)
    load_x.start()

    @pl.loop(0, n_ff)
    def _(j):
        pltpu.make_async_copy(wg_ref.at[:, ff_cols(j)], vg.at[:, ff_cols(j)], wgu_sem.at[j]).start()
        pltpu.make_async_copy(wu_ref.at[:, ff_cols(j)], vu.at[:, ff_cols(j)], wgu_sem.at[j]).start()

    load_down = pltpu.make_async_copy(wd_ref, vd, wd_sem)
    load_down.start()

    def remote(src, dst, send_sem, recv_sem, to):
        return pltpu.make_async_remote_copy(
            src_ref=src, dst_ref=dst, send_sem=send_sem, recv_sem=recv_sem,
            device_id={"tp": to}, device_id_type=MESH,
        )

    def wait_recv(block, sem):
        pltpu.make_async_copy(block, block, sem).wait()

    def wait_sent(block, sem):
        pltpu.make_async_copy(block, block, sem).wait()

    def gather_own():
        remote(x_ref.at[first], xg.at[1, first], ag_send, ag_recv.at[0], right).start()
        remote(x_ref.at[second], xg.at[1, second], ag_send, ag_recv.at[0], left).start()
        remote(x_ref.at[second], xg.at[2, first], ag_send, ag_recv.at[1], right).start()
        remote(x_ref.at[first], xg.at[2, second], ag_send, ag_recv.at[1], left).start()

    def gather_forward():
        remote(xg.at[1, first], xg.at[3, first], ag_send, ag_recv.at[2], right).start()
        remote(xg.at[1, second], xg.at[3, second], ag_send, ag_recv.at[2], left).start()

    def reduce_send(src, to_left, to_right, dst, at_left, at_right, sem, cols):
        remote(src.at[to_left, cols], dst.at[at_left, cols], rs_send, sem, left).start()
        remote(src.at[to_right, cols], dst.at[at_right, cols], rs_send, sem, right).start()

    def direct(j):
        reduce_send(xg.at[0], first, second, r_dir, first, second, dir_recv, out_cols(j))

    def hop(j):
        reduce_send(xg.at[3], second, first, r_hop, first, second, hop_recv.at[j], out_cols(j))

    def running(j):
        reduce_send(xg.at[2], first, second, r_run, second, first, run_recv.at[j], out_cols(j))

    pl.semaphore_wait(barrier, 2)
    gather_own()

    def hidden(group, out, loading):
        @pl.loop(0, n_ff)
        def _(j):
            if loading:
                both = pl.ds(0, 2 * FF_TILE)
                pltpu.make_async_copy(wg_ref.at[:, both], vg.at[:, both], wgu_sem.at[j]).wait()
            gate = jnp.dot(xg[group], vg[:, ff_cols(j)], preferred_element_type=jnp.float32)
            up = jnp.dot(xg[group], vu[:, ff_cols(j)], preferred_element_type=jnp.float32)
            out[:, ff_cols(j)] = (jax.nn.silu(gate) * up).astype(out.dtype)

    def down(src, j):
        return jnp.dot(src[...], vd[:, out_cols(j)], preferred_element_type=jnp.float32)

    load_x.wait()
    hidden(0, hid, True)
    load_down.wait()

    @pl.loop(0, n_out)
    def _(j):
        acc[:, out_cols(j)] = down(hid, j)

    wait_recv(xg.at[1], ag_recv.at[0])
    gather_forward()
    hidden(1, hid, False)

    @pl.loop(0, n_out)
    def _(j):
        xg[0, :, out_cols(j)] = down(hid, j).astype(xg.dtype)

        @pl.when(j > 0)
        def _():
            direct(j - 1)

    wait_recv(xg.at[2], ag_recv.at[1])
    direct(n_out - 1)
    hidden(2, hid2, False)

    wait_recv(xg.at[3], ag_recv.at[2])
    hidden(3, hid, False)

    @pl.loop(0, n_out)
    def _(j):
        xg[3, :, out_cols(j)] = down(hid, j).astype(xg.dtype)

        @pl.when(j > 0)
        def _():
            hop(j - 1)

    wait_recv(r_dir, dir_recv)
    hop(n_out - 1)

    @pl.loop(0, n_out)
    def _(j):
        acc[:, out_cols(j)] = acc[:, out_cols(j)] + r_dir[:, out_cols(j)].astype(jnp.float32)

    @pl.loop(0, n_out)
    def _(j):
        wait_recv(r_hop.at[:, out_cols(j)], hop_recv.at[j])
        total = down(hid2, j) + r_hop[:, out_cols(j)].astype(jnp.float32)
        xg[2, :, out_cols(j)] = total.astype(xg.dtype)

        @pl.when(j > 0)
        def _():
            running(j - 1)

    wait_sent(xg.at[pl.ds(0, 3)], ag_send)
    running(n_out - 1)

    @pl.loop(0, n_out)
    def _(j):
        wait_recv(r_run.at[:, out_cols(j)], run_recv.at[j])
        total = acc[:, out_cols(j)] + r_run[:, out_cols(j)].astype(jnp.float32)
        y_ref[:, out_cols(j)] = total.astype(y_ref.dtype)

    wait_sent(xg.at[pl.ds(0, 3)], rs_send)


def solution(mesh):
    n = mesh.shape["tp"]

    def step(x, w_gate, w_up, w_down):
        rows, d = x.shape
        ff = w_gate.shape[1]
        n_ff, n_out = ff // FF_TILE, d // OUT_TILE
        bf16, f32 = jnp.bfloat16, jnp.float32
        block = pltpu.VMEM((rows, d), bf16)
        sem = pltpu.SemaphoreType.DMA
        return pl.pallas_call(
            functools.partial(kernel, n),
            out_shape=pltpu.VMEM((rows, d), bf16),
            in_specs=[pl.BlockSpec(memory_space=pl.ANY)] * 4,
            out_specs=pl.BlockSpec(memory_space=pltpu.VMEM),
            scratch_shapes=[
                pltpu.VMEM((4, rows, d), bf16),
                pltpu.VMEM((d, ff), bf16), pltpu.VMEM((d, ff), bf16), pltpu.VMEM((ff, d), bf16),
                pltpu.VMEM((rows, d), f32),
                pltpu.VMEM((rows, ff), bf16), pltpu.VMEM((rows, ff), bf16),
                block, block, block,
                sem, sem((n_ff,)), sem, sem, sem((3,)), sem, sem, sem((n_out,)), sem((n_out,)),
            ],
            compiler_params=pltpu.CompilerParams(
                collective_id=0, has_side_effects=True, vmem_limit_bytes=58 * 2**20
            ),
        )(x, w_gate, w_up, w_down)

    return jax.shard_map(
        step,
        mesh=mesh,
        in_specs=(P(("dp", "tp"), None), P(None, "tp"), P(None, "tp"), P("tp", None)),
        out_specs=P(("dp", "tp"), None),
        check_vma=False,
    )
```

time: 149 us -> 146 us (0.980)
  Pallas kernels: 146 us -> 144 us
  local copies, waits for them, and re-layouts: 3.09 us -> 1.34 us
    unnamed x1, local copies, waits for them, and re-layouts: 3.09 us -> 1.34 us
    pallas_call x1, Pallas kernels: 146 us -> 144 us  [step(): pl.pallas_call(functools.partial(kernel, n), out_shape=pltpu.VMEM((rows,...]
where the time goes in v2:
time: 146 us
  Pallas kernels  144 us (99%)
    pallas_call x1, Pallas kernels, step(): pl.pallas_call(functools.partial(kernel, n), out_shape=pltpu.VMEM((rows,...  144 us

profile of v2, /device:TPU:112, one launch (start us, length us, event | category | flops | bytes accessed | tf_op | source)
XLA Modules:
  0.0 145.8 jit_solution(5406061878865532133)
XLA Ops:
  0.0 144.4 %shard_map.46 = bf16[352,3072]{1,0:T(8,128)(2,1)S(1)} custom-call(bf16[352,3072]{1,0:T(8,128)(2,1)} %x_ref.1, bf16[3072,2048]{1,0:T(8,128)(2,1)} %wg_ref.1, bf16[3072,2048]{1,0:T(8,128)(2,1)} %wu_ref.1, bf16[2048,3072]{1,0:T(8,128)(2,1)} %wd_ref.1), custom_call_target="tpu_custom_call" | custom-call | tf_op jit(solution)/shard_map/pallas_call | solution.py:174
  144.4 1.3 copy.6

commit v3 on v2

v3 whole, which is shorter than its diff:
```python
import functools

import jax
import jax.numpy as jnp
from jax import lax
from jax.experimental import pallas as pl
from jax.experimental.pallas import tpu as pltpu
from jax.sharding import PartitionSpec as P

MESH = pl.DeviceIdType.MESH
FF_TILE = 256
OUT_TILE = 512
LAST = 256
X, R_DIR, R_HOP, R_RUN = 0, 4, 5, 6


def kernel(
    n, x_ref, wg_ref, wu_ref, wd_ref, y_ref,
    blocks, vgu, vd, acc, hid, hid2,
    x_sem, wgu_sem, wd_sem, send_sem, ag_recv, dir_recv, hop_recv, run_recv,
):
    rows, d = x_ref.shape
    ff = wg_ref.shape[1]
    half = rows // 2
    n_ff, n_out = ff // FF_TILE, d // OUT_TILE
    me = lax.axis_index("tp")
    right, left = lax.rem(me + 1, n), lax.rem(me + n - 1, n)
    first, second = pl.ds(0, half), pl.ds(half, half)
    xg = [blocks.at[X + i] for i in range(4)]
    r_dir, r_hop, r_run = blocks.at[R_DIR], blocks.at[R_HOP], blocks.at[R_RUN]

    barrier = pltpu.get_barrier_semaphore()
    for neighbour in (left, right):
        pl.semaphore_signal(barrier, inc=1, device_id={"tp": neighbour}, device_id_type=MESH)

    def ff_cols(j):
        return pl.ds(pl.multiple_of(j * FF_TILE, FF_TILE), FF_TILE)

    def out_cols(j):
        return pl.ds(pl.multiple_of(j * OUT_TILE, OUT_TILE), OUT_TILE)

    def wait(block, sem):
        pltpu.make_async_copy(block, block, sem).wait()

    pltpu.make_async_copy(x_ref, xg[0], x_sem).start()
    pltpu.make_async_copy(wg_ref, vgu.at[0], wgu_sem).start()
    pltpu.make_async_copy(wu_ref, vgu.at[1], wgu_sem).start()
    pltpu.make_async_copy(wd_ref, vd, wd_sem).start()

    def remote(src, dst, recv_sem, to):
        pltpu.make_async_remote_copy(
            src_ref=src, dst_ref=dst, send_sem=send_sem, recv_sem=recv_sem,
            device_id={"tp": to}, device_id_type=MESH,
        ).start()

    def gather_own():
        remote(x_ref.at[first], xg[1].at[first], ag_recv.at[0], right)
        remote(x_ref.at[second], xg[1].at[second], ag_recv.at[0], left)
        remote(x_ref.at[second], xg[2].at[first], ag_recv.at[1], right)
        remote(x_ref.at[first], xg[2].at[second], ag_recv.at[1], left)

    def gather_forward():
        remote(xg[1].at[first], xg[3].at[first], ag_recv.at[2], right)
        remote(xg[1].at[second], xg[3].at[second], ag_recv.at[2], left)

    def direct(j):
        cols = out_cols(j)
        remote(xg[0].at[first, cols], r_dir.at[first, cols], dir_recv, left)
        remote(xg[0].at[second, cols], r_dir.at[second, cols], dir_recv, right)

    def hop(j):
        cols = out_cols(j)
        remote(xg[3].at[second, cols], r_hop.at[first, cols], hop_recv.at[j // 2], left)
        remote(xg[3].at[first, cols], r_hop.at[second, cols], hop_recv.at[j // 2], right)

    def running(cols, piece):
        remote(xg[2].at[first, cols], r_run.at[second, cols], run_recv.at[piece], left)
        remote(xg[2].at[second, cols], r_run.at[first, cols], run_recv.at[piece], right)

    pl.semaphore_wait(barrier, 2)
    gather_own()

    def hidden(group, out):
        @pl.loop(0, n_ff)
        def _(j):
            gate = jnp.dot(xg[group][...], vgu[0, :, ff_cols(j)], preferred_element_type=jnp.float32)
            up = jnp.dot(xg[group][...], vgu[1, :, ff_cols(j)], preferred_element_type=jnp.float32)
            out[:, ff_cols(j)] = (jax.nn.silu(gate) * up).astype(out.dtype)

    def down(src, j):
        return jnp.dot(src[...], vd[:, out_cols(j)], preferred_element_type=jnp.float32)

    wait(xg[0], x_sem)
    wait(vgu, wgu_sem)
    hidden(0, hid)
    wait(vd, wd_sem)

    @pl.loop(0, n_out)
    def _(j):
        acc[:, out_cols(j)] = down(hid, j)

    wait(xg[1], ag_recv.at[0])
    gather_forward()
    hidden(1, hid)

    @pl.loop(0, n_out)
    def _(j):
        xg[0][:, out_cols(j)] = down(hid, j).astype(blocks.dtype)

        @pl.when(j > 0)
        def _():
            direct(j - 1)

    wait(xg[2], ag_recv.at[1])
    direct(n_out - 1)
    hidden(2, hid2)

    wait(xg[3], ag_recv.at[2])
    hidden(3, hid)

    @pl.loop(0, n_out)
    def _(j):
        xg[3][:, out_cols(j)] = down(hid, j).astype(blocks.dtype)

        @pl.when(j > 0)
        def _():
            hop(j - 1)

    wait(r_dir, dir_recv)
    hop(n_out - 1)

    @pl.loop(0, n_out)
    def _(j):
        acc[:, out_cols(j)] = acc[:, out_cols(j)] + r_dir[:, out_cols(j)].astype(jnp.float32)

    @pl.loop(0, n_out)
    def _(j):
        @pl.when(lax.rem(j, 2) == 0)
        def _():
            both = pl.ds(pl.multiple_of(j * OUT_TILE, 2 * OUT_TILE), 2 * OUT_TILE)
            wait(r_hop.at[:, both], hop_recv.at[j // 2])

        total = down(hid2, j) + r_hop[:, out_cols(j)].astype(jnp.float32)
        xg[2][:, out_cols(j)] = total.astype(blocks.dtype)

        @pl.when(j > 0)
        def _():
            running(out_cols(j - 1), 0)

    running(pl.ds(d - OUT_TILE, OUT_TILE - LAST), 0)
    running(pl.ds(d - LAST, LAST), 1)

    def finish(cols):
        total = acc[:, cols] + r_run[:, cols].astype(jnp.float32)
        y_ref[:, cols] = total.astype(y_ref.dtype)

    early, last = pl.ds(0, d - LAST), pl.ds(d - LAST, LAST)
    wait(r_run.at[:, early], run_recv.at[0])

    @pl.loop(0, (d - LAST) // LAST)
    def _(j):
        finish(pl.ds(pl.multiple_of(j * LAST, LAST), LAST))

    wait(blocks.at[pl.ds(0, 6)], send_sem)
    wait(r_run.at[:, last], run_recv.at[1])
    finish(last)


def solution(mesh):
    n = mesh.shape["tp"]

    def step(x, w_gate, w_up, w_down):
        rows, d = x.shape
        ff = w_gate.shape[1]
        bf16, f32 = jnp.bfloat16, jnp.float32
        sem = pltpu.SemaphoreType.DMA
        return pl.pallas_call(
            functools.partial(kernel, n),
            out_shape=pltpu.VMEM((rows, d), bf16),
            in_specs=[pl.BlockSpec(memory_space=pl.ANY)] * 4,
            out_specs=pl.BlockSpec(memory_space=pltpu.VMEM),
            scratch_shapes=[
                pltpu.VMEM((7, rows, d), bf16),
                pltpu.VMEM((2, d, ff), bf16), pltpu.VMEM((ff, d), bf16),
                pltpu.VMEM((rows, d), f32),
                pltpu.VMEM((rows, ff), bf16), pltpu.VMEM((rows, ff), bf16),
                sem, sem, sem, sem, sem((3,)), sem, sem((d // OUT_TILE // 2,)), sem((2,)),
            ],
            compiler_params=pltpu.CompilerParams(
                collective_id=0, has_side_effects=True, vmem_limit_bytes=58 * 2**20
            ),
        )(x, w_gate, w_up, w_down)

    return jax.shard_map(
        step,
        mesh=mesh,
        in_specs=(P(("dp", "tp"), None), P(None, "tp"), P(None, "tp"), P("tp", None)),
        out_specs=P(("dp", "tp"), None),
        check_vma=False,
    )
```

time: 146 us -> 146 us (level)
  no operation moved by 1% of the time
where the time goes in v3:
time: 146 us
  Pallas kernels  144 us (99%)
    pallas_call x1, Pallas kernels, step(): pl.pallas_call(functools.partial(kernel, n), out_shape=pltpu.VMEM((rows,...  144 us

profile of v3, /device:TPU:112, one launch (start us, length us, event | category | flops | bytes accessed | tf_op | source)
XLA Modules:
  0.0 145.6 jit_solution(12190751439700719600)
XLA Ops:
  0.0 144.2 %shard_map.46 = bf16[352,3072]{1,0:T(8,128)(2,1)S(1)} custom-call(bf16[352,3072]{1,0:T(8,128)(2,1)} %x_ref.1, bf16[3072,2048]{1,0:T(8,128)(2,1)} %wg_ref.1, bf16[3072,2048]{1,0:T(8,128)(2,1)} %wu_ref.1, bf16[2048,3072]{1,0:T(8,128)(2,1)} %wd_ref.1), custom_call_target="tpu_custom_call" | custom-call | tf_op jit(solution)/shard_map/pallas_call | solution.py:177
  144.3 1.3 copy.6

commit v4 on v3

--- a/solution.py
+++ b/solution.py
@@ -17,7 +17,7 @@
 def kernel(
     n, x_ref, wg_ref, wu_ref, wd_ref, y_ref,
     blocks, vgu, vd, acc, hid, hid2,
-    x_sem, wgu_sem, wd_sem, send_sem, ag_recv, dir_recv, hop_recv, run_recv,
+    x_sem, wgu_sem, wd_sem, send_sem, ag_recv, dir_recv, hop_recv, run_recv, here_sem,
 ):
     rows, d = x_ref.shape
     ff = wg_ref.shape[1]
@@ -30,8 +30,7 @@
     r_dir, r_hop, r_run = blocks.at[R_DIR], blocks.at[R_HOP], blocks.at[R_RUN]
 
     barrier = pltpu.get_barrier_semaphore()
-    for neighbour in (left, right):
-        pl.semaphore_signal(barrier, inc=1, device_id={"tp": neighbour}, device_id_type=MESH)
+    pl.semaphore_signal(barrier, inc=1, device_id={"tp": left}, device_id_type=MESH)
 
     def ff_cols(j):
         return pl.ds(pl.multiple_of(j * FF_TILE, FF_TILE), FF_TILE)
@@ -53,10 +52,12 @@
             device_id={"tp": to}, device_id_type=MESH,
         ).start()
 
-    def gather_own():
+    def gather_right():
         remote(x_ref.at[first], xg[1].at[first], ag_recv.at[0], right)
+        remote(x_ref.at[second], xg[2].at[first], ag_recv.at[1], right)
+
+    def gather_left():
         remote(x_ref.at[second], xg[1].at[second], ag_recv.at[0], left)
-        remote(x_ref.at[second], xg[2].at[first], ag_recv.at[1], right)
         remote(x_ref.at[first], xg[2].at[second], ag_recv.at[1], left)
 
     def gather_forward():
@@ -77,8 +78,11 @@
         remote(xg[2].at[first, cols], r_run.at[second, cols], run_recv.at[piece], left)
         remote(xg[2].at[second, cols], r_run.at[first, cols], run_recv.at[piece], right)
 
-    pl.semaphore_wait(barrier, 2)
-    gather_own()
+    pl.semaphore_wait(barrier, 1)
+    pl.semaphore_signal(here_sem, inc=1, device_id={"tp": right}, device_id_type=MESH)
+    gather_right()
+    pl.semaphore_wait(here_sem, 1)
+    gather_left()
 
     def hidden(group, out):
         @pl.loop(0, n_ff)
@@ -185,6 +189,7 @@
                 pltpu.VMEM((rows, d), f32),
                 pltpu.VMEM((rows, ff), bf16), pltpu.VMEM((rows, ff), bf16),
                 sem, sem, sem, sem, sem((3,)), sem, sem((d // OUT_TILE // 2,)), sem((2,)),
+                pltpu.SemaphoreType.REGULAR,
             ],
             compiler_params=pltpu.CompilerParams(
                 collective_id=0, has_side_effects=True, vmem_limit_bytes=58 * 2**20

time: 146 us -> 145 us (level)
  no operation moved by 1% of the time
where the time goes in v4:
time: 145 us
  Pallas kernels  144 us (99%)
    pallas_call x1, Pallas kernels, step(): pl.pallas_call(functools.partial(kernel, n), out_shape=pltpu.VMEM((rows,...  144 us

profile of v4, /device:TPU:112, one launch (start us, length us, event | category | flops | bytes accessed | tf_op | source)
XLA Modules:
  0.0 145.2 jit_solution(9246374215748313372)
XLA Ops:
  0.0 143.8 %shard_map.46 = bf16[352,3072]{1,0:T(8,128)(2,1)S(1)} custom-call(bf16[352,3072]{1,0:T(8,128)(2,1)} %x_ref.1, bf16[3072,2048]{1,0:T(8,128)(2,1)} %wg_ref.1, bf16[3072,2048]{1,0:T(8,128)(2,1)} %wu_ref.1, bf16[2048,3072]{1,0:T(8,128)(2,1)} %wd_ref.1), custom_call_target="tpu_custom_call" | custom-call | tf_op jit(solution)/shard_map/pallas_call | solution.py:181
  143.9 1.3 copy.6

commit v5 on v4

--- a/solution.py
+++ b/solution.py
@@ -11,7 +11,7 @@
 FF_TILE = 256
 OUT_TILE = 512
 LAST = 256
-X, R_DIR, R_HOP, R_RUN = 0, 4, 5, 6
+X, R_DIR, R_HOP, R_RUN, S_DIR = 0, 4, 5, 6, 7
 
 
 def kernel(
@@ -27,7 +27,7 @@
     right, left = lax.rem(me + 1, n), lax.rem(me + n - 1, n)
     first, second = pl.ds(0, half), pl.ds(half, half)
     xg = [blocks.at[X + i] for i in range(4)]
-    r_dir, r_hop, r_run = blocks.at[R_DIR], blocks.at[R_HOP], blocks.at[R_RUN]
+    r_dir, r_hop, r_run, s_dir = (blocks.at[i] for i in (R_DIR, R_HOP, R_RUN, S_DIR))
 
     barrier = pltpu.get_barrier_semaphore()
     pl.semaphore_signal(barrier, inc=1, device_id={"tp": left}, device_id_type=MESH)
@@ -66,13 +66,13 @@
 
     def direct(j):
         cols = out_cols(j)
-        remote(xg[0].at[first, cols], r_dir.at[first, cols], dir_recv, left)
-        remote(xg[0].at[second, cols], r_dir.at[second, cols], dir_recv, right)
+        remote(s_dir.at[first, cols], r_dir.at[first, cols], dir_recv, left)
+        remote(s_dir.at[second, cols], r_dir.at[second, cols], dir_recv, right)
 
     def hop(j):
         cols = out_cols(j)
-        remote(xg[3].at[second, cols], r_hop.at[first, cols], hop_recv.at[j // 2], left)
-        remote(xg[3].at[first, cols], r_hop.at[second, cols], hop_recv.at[j // 2], right)
+        remote(xg[3].at[second, cols], r_hop.at[first, cols], hop_recv.at[j // 3], left)
+        remote(xg[3].at[first, cols], r_hop.at[second, cols], hop_recv.at[j // 3], right)
 
     def running(cols, piece):
         remote(xg[2].at[first, cols], r_run.at[second, cols], run_recv.at[piece], left)
@@ -94,29 +94,29 @@
     def down(src, j):
         return jnp.dot(src[...], vd[:, out_cols(j)], preferred_element_type=jnp.float32)
 
-    wait(xg[0], x_sem)
-    wait(vgu, wgu_sem)
-    hidden(0, hid)
-    wait(vd, wd_sem)
-
-    @pl.loop(0, n_out)
-    def _(j):
-        acc[:, out_cols(j)] = down(hid, j)
-
     wait(xg[1], ag_recv.at[0])
     gather_forward()
+    wait(vgu, wgu_sem)
+    wait(vd, wd_sem)
     hidden(1, hid)
 
     @pl.loop(0, n_out)
     def _(j):
-        xg[0][:, out_cols(j)] = down(hid, j).astype(blocks.dtype)
+        s_dir[:, out_cols(j)] = down(hid, j).astype(blocks.dtype)
 
         @pl.when(j > 0)
         def _():
             direct(j - 1)
 
+    wait(xg[0], x_sem)
+    hidden(0, hid)
+    direct(n_out - 1)
+
+    @pl.loop(0, n_out)
+    def _(j):
+        acc[:, out_cols(j)] = down(hid, j)
+
     wait(xg[2], ag_recv.at[1])
-    direct(n_out - 1)
     hidden(2, hid2)
 
     wait(xg[3], ag_recv.at[2])
@@ -139,10 +139,10 @@
 
     @pl.loop(0, n_out)
     def _(j):
-        @pl.when(lax.rem(j, 2) == 0)
-        def _():
-            both = pl.ds(pl.multiple_of(j * OUT_TILE, 2 * OUT_TILE), 2 * OUT_TILE)
-            wait(r_hop.at[:, both], hop_recv.at[j // 2])
+        @pl.when(lax.rem(j, 3) == 0)
+        def _():
+            three = pl.ds(pl.multiple_of(j * OUT_TILE, 3 * OUT_TILE), 3 * OUT_TILE)
+            wait(r_hop.at[:, three], hop_recv.at[j // 3])
 
         total = down(hid2, j) + r_hop[:, out_cols(j)].astype(jnp.float32)
         xg[2][:, out_cols(j)] = total.astype(blocks.dtype)
@@ -184,15 +184,15 @@
             in_specs=[pl.BlockSpec(memory_space=pl.ANY)] * 4,
             out_specs=pl.BlockSpec(memory_space=pltpu.VMEM),
             scratch_shapes=[
-                pltpu.VMEM((7, rows, d), bf16),
+                pltpu.VMEM((8, rows, d), bf16),
                 pltpu.VMEM((2, d, ff), bf16), pltpu.VMEM((ff, d), bf16),
                 pltpu.VMEM((rows, d), f32),
                 pltpu.VMEM((rows, ff), bf16), pltpu.VMEM((rows, ff), bf16),
-                sem, sem, sem, sem, sem((3,)), sem, sem((d // OUT_TILE // 2,)), sem((2,)),
+                sem, sem, sem, sem, sem((3,)), sem, sem((d // OUT_TILE // 3,)), sem((2,)),
                 pltpu.SemaphoreType.REGULAR,
             ],
             compiler_params=pltpu.CompilerParams(
-                collective_id=0, has_side_effects=True, vmem_limit_bytes=58 * 2**20
+                collective_id=0, has_side_effects=True, vmem_limit_bytes=60 * 2**20
             ),
         )(x, w_gate, w_up, w_down)
 

time: 145 us -> 145 us (level)
  no operation moved by 1% of the time
where the time goes in v5:
time: 145 us
  Pallas kernels  144 us (99%)
    pallas_call x1, Pallas kernels, step(): pl.pallas_call(functools.partial(kernel, n), out_shape=pltpu.VMEM((rows,...  144 us

profile of v5, /device:TPU:112, one launch (start us, length us, event | category | flops | bytes accessed | tf_op | source)
XLA Modules:
  0.0 145.2 jit_solution(7873252890665339649)
XLA Ops:
  0.0 143.8 %shard_map.46 = bf16[352,3072]{1,0:T(8,128)(2,1)S(1)} custom-call(bf16[352,3072]{1,0:T(8,128)(2,1)} %x_ref.1, bf16[3072,2048]{1,0:T(8,128)(2,1)} %wg_ref.1, bf16[3072,2048]{1,0:T(8,128)(2,1)} %wu_ref.1, bf16[2048,3072]{1,0:T(8,128)(2,1)} %wd_ref.1), custom_call_target="tpu_custom_call" | custom-call | tf_op jit(solution)/shard_map/pallas_call | solution.py:181
  143.8 1.3 copy.6
